TPU v7x, 32 devices: a whole 2x2x4 slice. The times are simulated.
32 devices in a mesh: band: 16 (over z, y, core), chan: 2 (over x).
Axes of the slice: x: 2, y: 2, z: 4, core: 2. Of those that a mesh axis runs over, the one named last changes fastest.
Arguments:
- fine_features: bfloat16 [2, 192, 128, 512], P(None, 'chan', 'band'), may hold values from -100 to 100
- coarse_level: bfloat16 [2, 256, 64, 256], P(None, 'chan', 'band'), may hold values from -100 to 100
- lat_weight: bfloat16 [256, 192], P('chan'), may hold values from -0.4375 to 0.4375
- lat_gain: bfloat16 [256], P('chan'), may hold values from 0.099609375 to 1.8984375
- lat_shift: bfloat16 [256], P('chan'), may hold values from -3 to 3
- out_weight: bfloat16 [3, 3, 256, 256], P(None, None, 'chan'), may hold values from -0.125 to 0.125
- out_gain: bfloat16 [256], P('chan'), may hold values from 0.099609375 to 1.8984375
- out_shift: bfloat16 [256], P('chan'), may hold values from -3 to 3
- mask_weight: bfloat16 [256, 256], P('chan'), may hold values from -0.375 to 0.375
- mask_bias: bfloat16 [256], P('chan'), may hold values from -1.796875 to 1.796875
- queries: bfloat16 [200, 256], replicated, may hold values from -128 to 128
Outputs:
- log_probs: float32 [2, 200, 128, 512], P(None, None, ('band', 'chan'))
All inputs are finite; a program needn't handle non-finite values.
Results may differ from a plain program's by a relative error of at most 0.0058.
Values may be sent and summed in bfloat16 or wider, within the bound.
A program may use at most 128 MiB of HBM per device.

v0:
```python
import jax
import jax.numpy as jnp
from jax import lax
from jax.sharding import PartitionSpec as P

D = 256
GROUPS = 32
epsilon = 1e-05


def extended_2(cells, sides, width):
    for axis, dim in sides:
        count = lax.axis_size(axis)
        ends = count - 1
        head = lax.slice_in_dim(cells, 0, width, axis=dim)
        tail = lax.slice_in_dim(cells, cells.shape[dim] - width, cells.shape[dim], axis=dim)
        cells = jnp.concatenate(
            [
                lax.ppermute(tail, axis, [(i, (i + 1) % count) for i in range(ends)]),
                cells,
                lax.ppermute(head, axis, [((i + 1) % count, i) for i in range(ends)]),
            ],
            axis=dim,
        )
    return cells


def interp(padded, axis):
    length = padded.shape[axis] - 2
    before = lax.slice_in_dim(padded, 0, length, axis=axis)
    middle = lax.slice_in_dim(padded, 1, length + 1, axis=axis)
    after = lax.slice_in_dim(padded, 2, length + 2, axis=axis)
    even_part = 0.25 * before + 0.75 * middle
    odd_part = 0.75 * middle + 0.25 * after
    paired = jnp.stack([even_part, odd_part], axis + 1)
    new_shape = list(middle.shape)
    new_shape[axis] = 2 * length
    return paired.reshape(new_shape)


def conv_taps(taps_weight, padded, row_count, col_count):
    summed = None
    for row_tap in range(3):
        for col_tap in range(3):
            window = padded[:, :, row_tap : row_tap + row_count, col_tap : col_tap + col_count]
            term = jnp.einsum(
                "oc,ncrw->norw",
                taps_weight[row_tap, col_tap],
                window,
                preferred_element_type=jnp.float32,
            )
            summed = term if summed is None else summed + term
    return summed


def apply_norm(blocks, mean_value, variance, full_shape, gain, shift):
    scaled = (
        (blocks - mean_value[:, :, None]) * lax.rsqrt(variance[:, :, None] + epsilon)
    ).reshape(full_shape)
    return (
        scaled * gain.astype(jnp.float32)[None, :, None, None]
        + shift.astype(jnp.float32)[None, :, None, None]
    )


def per_device(
    fine_features,
    coarse_level,
    lat_weight,
    lat_gain,
    lat_shift,
    out_weight,
    out_gain,
    out_shift,
    mask_weight,
    mask_bias,
    queries,
):
    images, in_share, band_rows, columns = fine_features.shape
    out_share = lat_weight.shape[0]
    group_size = D // GROUPS
    band_count = lax.axis_size("band")
    pixel_count = float(group_size * band_rows * band_count * columns)
    lateral = jnp.einsum(
        "oc,ncrw->norw",
        lat_weight,
        lax.all_gather(fine_features, "chan", axis=1, tiled=True),
        preferred_element_type=jnp.float32,
    )
    lat_blocks = lateral.reshape(images, out_share // group_size, -1)
    lat_mean = lax.psum(jnp.sum(lat_blocks, 2), "band") / pixel_count
    deviation = lat_blocks - lat_mean[:, :, None]
    lat_var = lax.psum(jnp.sum(deviation * deviation, 2), "band") / pixel_count
    lat_normed = apply_norm(lat_blocks, lat_mean, lat_var, lateral.shape, lat_gain, lat_shift)
    band_index = lax.axis_index("band")
    extended = extended_2(coarse_level, (("band", 2),), 1)
    top_row = jnp.where(band_index == 0, extended[:, :, 1:2], extended[:, :, 0:1])
    bottom_row = jnp.where(band_index == band_count - 1, extended[:, :, -2:-1], extended[:, :, -1:])
    extended = jnp.concatenate([top_row, extended[:, :, 1:-1], bottom_row], 2).astype(jnp.float32)
    extended = jnp.pad(extended, ((0, 0), (0, 0), (0, 0), (1, 1)), mode="edge")
    upsampled = interp(interp(extended, 2), 3)
    joined = (lat_normed + upsampled).astype(jnp.bfloat16)
    row_joined = lax.all_to_all(joined, "chan", split_axis=2, concat_axis=1, tiled=True)
    conv_weight, full_gain, full_shift, full_mask, full_bias = (
        lax.all_gather(out_weight, "chan", axis=2, tiled=True),
        lax.all_gather(out_gain, "chan", axis=0, tiled=True),
        lax.all_gather(out_shift, "chan", axis=0, tiled=True),
        lax.all_gather(mask_weight, "chan", axis=0, tiled=True),
        lax.all_gather(mask_bias, "chan", axis=0, tiled=True),
    )
    row_count = row_joined.shape[2]
    padded = extended_2(row_joined, ((("band", "chan"), 2),), 1)
    padded = jnp.pad(padded, ((0, 0), (0, 0), (0, 0), (1, 1)))
    conv_out = conv_taps(conv_weight, padded, row_count, columns)
    local_groups = conv_out.shape[1] // group_size
    conv_blocks = conv_out.reshape(images, local_groups, -1)
    out_mean = lax.psum(jnp.sum(conv_blocks, 2), ("band", "chan")) / pixel_count
    deviation = conv_blocks - out_mean[:, :, None]
    out_var = lax.psum(jnp.sum(deviation * deviation, 2), ("band", "chan")) / pixel_count
    activated = jnp.maximum(
        apply_norm(conv_blocks, out_mean, out_var, conv_out.shape, full_gain, full_shift), 0.0
    ).astype(jnp.bfloat16)
    mixed = jnp.einsum("oc,ncrw->norw", full_mask, activated, preferred_element_type=jnp.float32)
    features = (mixed + full_bias.astype(jnp.float32)[None, :, None, None]).astype(jnp.bfloat16)
    logits = jnp.einsum("qc,ncrw->nqrw", queries, features, preferred_element_type=jnp.float32)
    peak = jnp.max(logits, axis=1, keepdims=True)
    shifted = logits - peak
    return shifted - jnp.log(jnp.sum(jnp.exp(shifted), axis=1, keepdims=True))


def solution(mesh):
    return jax.shard_map(
        per_device,
        mesh=mesh,
        in_specs=(
            P(None, "chan", "band", None),
            P(None, "chan", "band", None),
            P("chan", None),
            P("chan"),
            P("chan"),
            P(None, None, "chan", None),
            P("chan"),
            P("chan"),
            P("chan", None),
            P("chan"),
            P(),
        ),
        out_specs=P(None, None, ("band", "chan"), None),
        check_vma=False,
    )
```

profile of v0, /device:TPU:0, one launch (start us, length us, event | category | flops | bytes accessed | tf_op | source)
XLA Modules:
  0.0 355.2 jit_solution(3142790244294858030)
XLA Ops:
  6.6 3.1 copy.21
  13.9 4.2 %collective-permute-done.1 = bf16[2,128,1,256]{3,2,1,0:T(2,128)(2,1)S(1)} collective-permute-done((bf16[2,128,1,256]{3,2,1,0:T(2,128)(2,1)S(1)}, bf16[2,128,1,256]{3,2,1,0:T(2,128)(2,1)S(1)}, u32[]{:S(2)}, u32[]{:S(2)}) %collective-permute-start.1) | collective-permute-done | bytes 131104 | tf_op jit(solution)/shard_map/ppermute | solution.py:21
  24.6 3.2 copy.22
  28.8 5.2 %copy.23 = f32[2,128,8,256,2]{1,4,3,2,0:T(2,128)} copy(f32[2,128,8,256,2]{1,3,2,0,4:T(8,128)S(1)} %pad_maximum_fusion) | data formatting | bytes 8388608 | tf_op jit(solution)/shard_map/stack | solution.py:35
  34.0 23.6 %all-gather.6.cloned.1.call-done = bf16[2,192,8,512]{3,1,2,0:T(8,128)(2,1)} async-done(((bf16[2,96,8,512]{3,1,2,0:T(8,128)(2,1)}), bf16[2,192,8,512]{3,1,2,0:T(8,128)(2,1)}) %all-gather.6.cloned.1.call-update) | async-done | bytes 3145744 | tf_op jit(solution)/shard_map/all_gather | solution.py:87
  57.5 5.4 %bitcast_reduce_fusion.1 = (f32[2,128]{1,0:T(2,128)S(1)}, f32[2,8,512,128]{3,2,1,0:T(8,128)}) fusion(bf16[2,192,8,512]{3,1,2,0:T(8,128)(2,1)} %all-gather.6.cloned.1.call-done, bf16[128,192]{0,1:T(8,128)(2,1)S(1)} %copy-done.5), kind=kOutput, calls=%fused_computation.7 | convolution fusion | flops 403701504 | bytes 7390208 | tf_op jit(solution)/shard_map/oc,ncrw->norw/dot_general | solution.py:84
  63.1 33.2 %psum.28 = f32[2,16]{1,0:T(2,128)S(1)} all-reduce(f32[2,16]{1,0:T(2,128)S(1)} %reduce_sum.59), channel_id=1, replica_groups=mesh['band'=16,'chan'=2] {'band'}, use_global_device_ids=true, to_apply=%region_2.0 | all-reduce | flops 32 | bytes 256 | tf_op jit(solution)/shard_map/psum | solution.py:91
  96.5 2.8 multiply_reduce_fusion.1
  99.4 29.5 %psum.29 = f32[2,16]{1,0:T(2,128)S(1)} all-reduce(f32[2,16]{1,0:T(2,128)S(1)} %reduce_sum.62), channel_id=1, replica_groups=mesh['band'=16,'chan'=2] {'band'}, use_global_device_ids=true, to_apply=%region_5.6 | all-reduce | flops 32 | bytes 256 | tf_op jit(solution)/shard_map/psum | solution.py:93
  129.0 4.3 %add_convert_fusion.1 = bf16[2,128,8,512]{1,3,2,0:T(8,128)(2,1)S(1)} fusion(f32[2,128,8,512]{1,3,2,0:T(8,128)} %bitcast.138, f32[2,8,512,128]{3,2,1,0:T(8,128)} %get-tuple-element.18, f32[128]{0:T(128)S(1)} %convert_element_type.33, f32[128]{0:T(128)S(1)} %convert_element_type.32, f32[2,128]{1,0:T(2,128)S(1)} %mul.72, f32[2,128]{1,0:T(2,128)S(1)} %sub.53), kind=kLoop, calls=%fused_computation.12 | loop fusion | flops 6291456 | bytes 10488832 | tf_op jit(solution)/shard_map/convert_element_type | solution.py:102
  134.9 3.8 %all-to-all-start = ((bf16[2,128,8,512]{1,3,0,2:T(8,128)(2,1)}), bf16[2,128,8,512]{1,3,0,2:T(8,128)(2,1)S(1)}, u32[]{:S(2)}, u32[]{:S(2)}) async-start(bf16[2,128,8,512]{1,3,0,2:T(8,128)(2,1)} %copy.24), calls=%async_computation | async-start | bytes 4194304 | tf_op jit(solution)/shard_map/all_to_all | solution.py:103
  139.4 37.0 %all-to-all-done = bf16[2,128,8,512]{1,3,0,2:T(8,128)(2,1)S(1)} async-done(((bf16[2,128,8,512]{1,3,0,2:T(8,128)(2,1)}), bf16[2,128,8,512]{1,3,0,2:T(8,128)(2,1)S(1)}, u32[]{:S(2)}, u32[]{:S(2)}) %all-to-all-start) | async-done | bytes 2097184 | tf_op jit(solution)/shard_map/all_to_all | solution.py:103
  176.4 3.5 copy.42
  179.9 3.2 all_to_all.16
  186.4 11.5 %all-gather = bf16[2,1,128]{2,1,0:T(2,128)(2,1)S(1)} all-gather(bf16[1,1,128]{2,1,0:T(2,128)(2,1)S(1)} %bitcast.144), channel_id=1, replica_groups=mesh['band'=16,'chan'=2] {'chan'}, dimensions={0}, use_global_device_ids=true | all-gather | bytes 768 | tf_op jit(solution)/shard_map/all_gather | solution.py:106
  198.0 4.2 %all-gather.1 = bf16[2,1,128]{2,1,0:T(2,128)(2,1)S(1)} all-gather(bf16[1,1,128]{2,1,0:T(2,128)(2,1)S(1)} %bitcast.145), channel_id=1, replica_groups=mesh['band'=16,'chan'=2] {'chan'}, dimensions={0}, use_global_device_ids=true | all-gather | bytes 768 | tf_op jit(solution)/shard_map/all_gather | solution.py:107
  202.2 4.2 %all-gather.2 = bf16[2,1,128]{2,1,0:T(2,128)(2,1)S(1)} all-gather(bf16[1,1,128]{2,1,0:T(2,128)(2,1)S(1)} %bitcast.146), channel_id=1, replica_groups=mesh['band'=16,'chan'=2] {'chan'}, dimensions={0}, use_global_device_ids=true | all-gather | bytes 768 | tf_op jit(solution)/shard_map/all_gather | solution.py:109
  206.4 4.9 %all_gather.22 = bf16[256,256]{1,0:T(8,128)(2,1)S(1)} all-gather(bf16[128,256]{1,0:T(8,128)(2,1)S(1)} %copy-done.4), channel_id=1, replica_groups=mesh['band'=16,'chan'=2] {'chan'}, dimensions={0}, use_global_device_ids=true | all-gather | bytes 196608 | tf_op jit(solution)/shard_map/all_gather | solution.py:108
  214.5 2.7 fusion.7
  217.2 9.8 %collective-permute-done.3 = bf16[2,256,1,512]{1,3,2,0:T(8,128)(2,1)S(1)} collective-permute-done((bf16[2,256,1,512]{1,3,2,0:T(8,128)(2,1)}, bf16[2,256,1,512]{1,3,2,0:T(8,128)(2,1)S(1)}, u32[]{:S(2)}, u32[]{:S(2)}) %collective-permute-start.3) | collective-permute-done | bytes 524320 | tf_op jit(solution)/shard_map/ppermute | solution.py:21
  227.9 2.7 fusion.11
  230.6 2.7 fusion.19
  233.3 2.7 fusion.21
  236.0 2.7 fusion.23
  238.7 2.7 fusion.25
  241.5 2.8 fusion.27
  244.9 11.3 %bitcast_reduce_fusion = (f32[2,256]{1,0:T(2,128)S(1)}, f32[2,4,512,256]{3,2,1,0:T(8,128)}) fusion(bf16[3,3,256,256]{3,2,1,0:T(8,128)(2,1)} %all-gather.8.cloned.1.call-done, bf16[2,256,6,514]{1,3,2,0:T(8,128)(2,1)S(1)} %fusion.6, f32[2,4,512,256]{3,2,1,0:T(8,128)} %fusion.11, f32[2,4,512,256]{3,2,1,0:T(8,128)} %fusion.19, f32[2,4,512,256]{3,2,1,0:T(8,128)} %fusion.21, ...), kind=kOutput, calls=%fused_computation.5 | convolution fusion | flops 546307584 | bytes 39979008 | tf_op jit(solution)/shard_map/oc,ncrw->norw/dot_general | solution.py:46
  256.4 37.0 %psum.30 = f32[2,32]{1,0:T(2,128)S(1)} all-reduce(f32[2,32]{1,0:T(2,128)S(1)} %reduce_sum.81), channel_id=1, replica_groups=mesh['band'=16,'chan'=2] {'band','chan'}, use_global_device_ids=true, to_apply=%region_8.9 | all-reduce | flops 64 | bytes 512 | tf_op jit(solution)/shard_map/psum | solution.py:117
  296.4 40.9 %psum.31 = f32[2,32]{1,0:T(2,128)S(1)} all-reduce(f32[2,32]{1,0:T(2,128)S(1)} %reduce_sum.84), channel_id=1, replica_groups=mesh['band'=16,'chan'=2] {'band','chan'}, use_global_device_ids=true, to_apply=%region_11.12 | all-reduce | flops 64 | bytes 512 | tf_op jit(solution)/shard_map/psum | solution.py:119
  337.5 3.7 %fusion.33 = f32[2,4,512,200]{2,3,1,0:T(8,128)S(1)} fusion(f32[2,4,512,256]{3,2,1,0:T(8,128)} %get-tuple-element.20, f32[256]{0:T(256)S(1)} %bitcast.143, f32[256]{0:T(256)S(1)} %bitcast.142, f32[256]{0:T(256)S(1)} %bitcast.141, f32[2,256]{1,0:T(2,128)S(1)} %mul.85, f32[2,256]{1,0:T(2,128)S(1)} %sub.57, bf16[256,256]{1,0:T(8,128)(2,1)S(1)} %all_gather.22, ...), kind=kOutput, calls=%fused_computation.52 | convolution fusion | flops 964689920 | bytes 7711744 | tf_op jit(solution)/shard_map/qc,ncrw->nqrw/dot_general | solution.py:125
  341.2 2.9 exponential_reduce_fusion
  344.6 3.8 %copy.27 = f32[2,200,4,512]{3,2,1,0:T(4,128)} copy(f32[2,200,4,512]{3,1,2,0:T(8,128)S(1)} %log_subtract_fusion) | data formatting | bytes 6553600 | tf_op jit(solution)/shard_map/sub | solution.py:128
  (73 shorter events, 26.3 us)
Async XLA Ops:
  6.5 331.0 %copy-start = (bf16[200,256]{1,0:T(8,128)(2,1)S(1)}, bf16[200,256]{1,0:T(8,128)(2,1)}, u32[]{:S(2)}) copy-start(bf16[200,256]{1,0:T(8,128)(2,1)} %param.21) | copy-start | bytes 307204
  6.5 3.2 copy-start.2
  6.5 7.3 %copy-start.6 = (bf16[128]{0:T(256)(128)(2,1)S(1)}, bf16[128]{0:T(256)(128)(2,1)}, u32[]{:S(2)}) copy-start(bf16[128]{0:T(256)(128)(2,1)} %param.14) | copy-start | bytes 772
  6.5 7.3 %copy-start.7 = (bf16[128]{0:T(256)(128)(2,1)S(1)}, bf16[128]{0:T(256)(128)(2,1)}, u32[]{:S(2)}) copy-start(bf16[128]{0:T(256)(128)(2,1)} %param.15) | copy-start | bytes 772
  6.5 51.0 %all-gather.6.cloned.1.call-start = ((), (), s32[]{:S(2)}) async-start(), calls=%async_computation.1 | async-start | bytes 4718592 | tf_op jit(solution)/shard_map/all_gather | solution.py:87
  10.1 3.8 %collective-permute-start = (bf16[2,128,1,256]{3,2,1,0:T(2,128)(2,1)S(1)}, bf16[2,128,1,256]{3,2,1,0:T(2,128)(2,1)S(1)}, u32[]{:S(2)}, u32[]{:S(2)}) collective-permute-start(bf16[2,128,1,256]{3,2,1,0:T(2,128)(2,1)S(1)} %get-tuple-element.15), channel_id=1, source_target_pairs={{0,2},{2,4},{4,6},{6,8},{8,10},{10,12},{12,14},{14,16},{16,18},{18... | collective-permute-start | bytes 393224 | tf_op jit(solution)/shard_map/ppermute | solution.py:19
  12.6 5.5 %collective-permute-start.1 = (bf16[2,128,1,256]{3,2,1,0:T(2,128)(2,1)S(1)}, bf16[2,128,1,256]{3,2,1,0:T(2,128)(2,1)S(1)}, u32[]{:S(2)}, u32[]{:S(2)}) collective-permute-start(bf16[2,128,1,256]{3,2,1,0:T(2,128)(2,1)S(1)} %get-tuple-element.16), channel_id=1, source_target_pairs={{2,0},{4,2},{6,4},{8,6},{10,8},{12,10},{14,12},{16,14},{18,16},{20... | collective-permute-start | bytes 393224 | tf_op jit(solution)/shard_map/ppermute | solution.py:21
  28.8 28.8 %copy-start.5 = (bf16[128,192]{0,1:T(8,128)(2,1)S(1)}, bf16[128,192]{0,1:T(8,128)(2,1)}, u32[]{:S(2)}) copy-start(bf16[128,192]{0,1:T(8,128)(2,1)} %param.13) | copy-start | bytes 147460
  134.9 41.5 %all-to-all-start = ((bf16[2,128,8,512]{1,3,0,2:T(8,128)(2,1)}), bf16[2,128,8,512]{1,3,0,2:T(8,128)(2,1)S(1)}, u32[]{:S(2)}, u32[]{:S(2)}) async-start(bf16[2,128,8,512]{1,3,0,2:T(8,128)(2,1)} %copy.24), calls=%async_computation | async-start | bytes 4194304 | tf_op jit(solution)/shard_map/all_to_all | solution.py:103
  138.6 74.0 %all-gather.8.cloned.1.call-start = ((), (), s32[]{:S(2)}) async-start(), calls=%async_computation.2 | async-start | bytes 1769472 | tf_op jit(solution)/shard_map/all_gather | solution.py:105
  179.9 6.5 %copy-start.8 = (bf16[128]{0:T(256)(128)(2,1)S(1)}, bf16[128]{0:T(256)(128)(2,1)}, u32[]{:S(2)}) copy-start(bf16[128]{0:T(256)(128)(2,1)} %param.17) | copy-start | bytes 772
  179.9 18.1 %copy-start.9 = (bf16[128]{0:T(256)(128)(2,1)S(1)}, bf16[128]{0:T(256)(128)(2,1)}, u32[]{:S(2)}) copy-start(bf16[128]{0:T(256)(128)(2,1)} %param.18) | copy-start | bytes 772
  179.9 22.3 %copy-start.10 = (bf16[128]{0:T(256)(128)(2,1)S(1)}, bf16[128]{0:T(256)(128)(2,1)}, u32[]{:S(2)}) copy-start(bf16[128]{0:T(256)(128)(2,1)} %param.20) | copy-start | bytes 772
  179.9 26.6 %copy-start.4 = (bf16[128,256]{1,0:T(8,128)(2,1)S(1)}, bf16[128,256]{1,0:T(8,128)(2,1)}, u32[]{:S(2)}) copy-start(bf16[128,256]{1,0:T(8,128)(2,1)} %param.19) | copy-start | bytes 196612
  184.2 30.2 %collective-permute-start.2 = (bf16[2,256,1,512]{1,3,2,0:T(8,128)(2,1)}, bf16[2,256,1,512]{1,3,2,0:T(8,128)(2,1)S(1)}, u32[]{:S(2)}, u32[]{:S(2)}) collective-permute-start(bf16[2,256,1,512]{1,3,2,0:T(8,128)(2,1)} %get-tuple-element.9), channel_id=1, source_target_pairs={{0,1},{1,2},{2,3},{3,4},{4,5},{5,6},{6,7},{7,8},{8,9},{9,10},{10,1... | collective-permute-start | bytes 1572872 | tf_op jit(solution)/shard_map/ppermute | solution.py:19
  211.4 15.6 %collective-permute-start.3 = (bf16[2,256,1,512]{1,3,2,0:T(8,128)(2,1)}, bf16[2,256,1,512]{1,3,2,0:T(8,128)(2,1)S(1)}, u32[]{:S(2)}, u32[]{:S(2)}) collective-permute-start(bf16[2,256,1,512]{1,3,2,0:T(8,128)(2,1)} %get-tuple-element.10), channel_id=1, source_target_pairs={{1,0},{2,1},{3,2},{4,3},{5,4},{6,5},{7,6},{8,7},{9,8},{10,9},{11,1... | collective-permute-start | bytes 1572872 | tf_op jit(solution)/shard_map/ppermute | solution.py:21
  212.7 1.8 copy-start.3
  241.5 3.4 copy-start.1
Sparse Core Ops, SparseCore 0:
  9.9 47.6 all-gather.5
  141.0 33.2 all-gather.7
where the time goes:
time: 356 us; the launch traced here: 355 us
  blocking collectives  166 us (47%)
  waiting for transfers between devices  75.2 us (21%)
  matrix products  41.1 us (12%)
  local copies, waits for them, and re-layouts  27.1 us (8%)
  other arithmetic  21.5 us (6%)
  between operations  13.7 us (4%)
  starting transfers between devices  11 us (3%)
    psum x1, blocking collectives, per_device(): lax.psum(jnp.sum(deviation * deviation, 2), ('band', 'chan')) / pixel_count  40.9 us
    psum x1, blocking collectives, per_device(): out_mean = lax.psum(jnp.sum(conv_blocks, 2), ('band', 'chan')) / pixel_count  37 us
    all_to_all x1, waiting for transfers between devices, per_device(): lax.all_to_all(joined, 'chan', split_axis=2, concat_axis=1, tiled=True)  37 us
    psum x1, blocking collectives, per_device(): lat_mean = lax.psum(jnp.sum(lat_blocks, 2), 'band') / pixel_count  33.2 us
    dot_general x9, matrix products, conv_taps(): jnp.einsum('oc,ncrw->norw', taps_weight[row_tap, col_tap], window, prefer...  32.1 us
    psum x1, blocking collectives, per_device(): lat_var = lax.psum(jnp.sum(deviation * deviation, 2), 'band') / pixel_count  29.5 us
    all_gather x1, waiting for transfers between devices, per_device(): lax.all_gather(fine_features, 'chan', axis=1, tiled=True)  23.6 us
    ppermute x2, waiting for transfers between devices, extended_2(): lax.ppermute(head, axis, [((i + 1) % count, i) for i in range(ends)])  13.9 us
  transfers between devices with their start and end apart: 7, of which 4 were waited for; matrix products, arithmetic and copies ran while one was open for 7% of the time, Pallas kernels for 0%

commit v1 on v0

--- a/solution.py
+++ b/solution.py
@@ -2,10 +2,16 @@
 import jax.numpy as jnp
 from jax import lax
 from jax.sharding import PartitionSpec as P
+from jax.lax import all_gather
 
 D = 256
 GROUPS = 32
 epsilon = 1e-05
+
+
+def floor_render(mat, mesh_ax):
+    row_out = all_gather(mat, axis_name=mesh_ax)
+    return jnp.sum(row_out, 0)
 
 
 def extended_2(cells, sides, width):
@@ -116,7 +122,7 @@
     conv_blocks = conv_out.reshape(images, local_groups, -1)
     out_mean = lax.psum(jnp.sum(conv_blocks, 2), ("band", "chan")) / pixel_count
     deviation = conv_blocks - out_mean[:, :, None]
-    out_var = lax.psum(jnp.sum(deviation * deviation, 2), ("band", "chan")) / pixel_count
+    out_var = floor_render(jnp.sum(deviation * deviation, 2), ("band", "chan")) / pixel_count
     activated = jnp.maximum(
         apply_norm(conv_blocks, out_mean, out_var, conv_out.shape, full_gain, full_shift), 0.0
     ).astype(jnp.bfloat16)

time: 356 us -> 381 us (1.070)
  blocking collectives: 166 us -> 191 us
    all_gather x0 -> x1, blocking collectives: none -> 66.1 us  [floor_render(): row_out = all_gather(mat, axis_name=mesh_ax)]
    psum x1 -> x0, blocking collectives: 40.9 us -> none  [per_device(): lax.psum(jnp.sum(deviation * deviation, 2), ('band', 'chan')) / pixel_count]
where the time goes in v1:
time: 381 us; the launch traced here: 380 us
  blocking collectives  191 us (50%)
  waiting for transfers between devices  75.2 us (20%)
  matrix products  41.1 us (11%)
  local copies, waits for them, and re-layouts  27.1 us (7%)
  other arithmetic  21.6 us (6%)
  between operations  13.7 us (4%)
  starting transfers between devices  11 us (3%)
    all_gather x1, blocking collectives, floor_render(): row_out = all_gather(mat, axis_name=mesh_ax)  66.1 us
    psum x1, blocking collectives, per_device(): out_mean = lax.psum(jnp.sum(conv_blocks, 2), ('band', 'chan')) / pixel_count  37 us
    all_to_all x1, waiting for transfers between devices, per_device(): lax.all_to_all(joined, 'chan', split_axis=2, concat_axis=1, tiled=True)  37 us
    psum x1, blocking collectives, per_device(): lat_mean = lax.psum(jnp.sum(lat_blocks, 2), 'band') / pixel_count  33.2 us
    dot_general x9, matrix products, conv_taps(): jnp.einsum('oc,ncrw->norw', taps_weight[row_tap, col_tap], window, prefer...  32.1 us
    psum x1, blocking collectives, per_device(): lat_var = lax.psum(jnp.sum(deviation * deviation, 2), 'band') / pixel_count  29.5 us
    all_gather x1, waiting for transfers between devices, per_device(): lax.all_gather(fine_features, 'chan', axis=1, tiled=True)  23.6 us
    ppermute x2, waiting for transfers between devices, extended_2(): lax.ppermute(head, axis, [((i + 1) % count, i) for i in range(ends)])  13.9 us
  transfers between devices with their start and end apart: 7, of which 4 were waited for; matrix products, arithmetic and copies ran while one was open for 7% of the time, Pallas kernels for 0%

profile of v1, /device:TPU:0, one launch (start us, length us, event | category | flops | bytes accessed | tf_op | source)
XLA Modules:
  0.0 380.4 jit_solution(7835147488105375304)
XLA Ops:
  6.6 3.1 copy.21
  13.9 4.2 %collective-permute-done.1 = bf16[2,128,1,256]{3,2,1,0:T(2,128)(2,1)S(1)} collective-permute-done((bf16[2,128,1,256]{3,2,1,0:T(2,128)(2,1)S(1)}, bf16[2,128,1,256]{3,2,1,0:T(2,128)(2,1)S(1)}, u32[]{:S(2)}, u32[]{:S(2)}) %collective-permute-start.1) | collective-permute-done | bytes 131104 | tf_op jit(solution)/shard_map/ppermute | solution.py:27
  24.6 3.2 copy.22
  28.8 5.2 %copy.23 = f32[2,128,8,256,2]{1,4,3,2,0:T(2,128)} copy(f32[2,128,8,256,2]{1,3,2,0,4:T(8,128)S(1)} %pad_maximum_fusion) | data formatting | bytes 8388608 | tf_op jit(solution)/shard_map/stack | solution.py:41
  34.0 23.6 %all-gather.8.cloned.1.call-done = bf16[2,192,8,512]{3,1,2,0:T(8,128)(2,1)} async-done(((bf16[2,96,8,512]{3,1,2,0:T(8,128)(2,1)}), bf16[2,192,8,512]{3,1,2,0:T(8,128)(2,1)}) %all-gather.8.cloned.1.call-update) | async-done | bytes 3145744 | tf_op jit(solution)/shard_map/all_gather | solution.py:93
  57.5 5.4 %bitcast_reduce_fusion.1 = (f32[2,128]{1,0:T(2,128)S(1)}, f32[2,8,512,128]{3,2,1,0:T(8,128)}) fusion(bf16[2,192,8,512]{3,1,2,0:T(8,128)(2,1)} %all-gather.8.cloned.1.call-done, bf16[128,192]{0,1:T(8,128)(2,1)S(1)} %copy-done.5), kind=kOutput, calls=%fused_computation.7 | convolution fusion | flops 403701504 | bytes 7390208 | tf_op jit(solution)/shard_map/oc,ncrw->norw/dot_general | solution.py:90
  63.1 33.2 %psum.21 = f32[2,16]{1,0:T(2,128)S(1)} all-reduce(f32[2,16]{1,0:T(2,128)S(1)} %reduce_sum.67), channel_id=1, replica_groups=mesh['band'=16,'chan'=2] {'band'}, use_global_device_ids=true, to_apply=%region_2.0 | all-reduce | flops 32 | bytes 256 | tf_op jit(solution)/shard_map/psum | solution.py:97
  96.5 2.8 multiply_reduce_fusion.1
  99.4 29.5 %psum.22 = f32[2,16]{1,0:T(2,128)S(1)} all-reduce(f32[2,16]{1,0:T(2,128)S(1)} %reduce_sum.73), channel_id=1, replica_groups=mesh['band'=16,'chan'=2] {'band'}, use_global_device_ids=true, to_apply=%region_5.6 | all-reduce | flops 32 | bytes 256 | tf_op jit(solution)/shard_map/psum | solution.py:99
  129.0 4.3 %add_convert_fusion.1 = bf16[2,128,8,512]{1,3,2,0:T(8,128)(2,1)S(1)} fusion(f32[2,128,8,512]{1,3,2,0:T(8,128)} %bitcast.139, f32[2,8,512,128]{3,2,1,0:T(8,128)} %get-tuple-element.18, f32[128]{0:T(128)S(1)} %convert_element_type.33, f32[128]{0:T(128)S(1)} %convert_element_type.32, f32[2,128]{1,0:T(2,128)S(1)} %mul.72, f32[2,128]{1,0:T(2,128)S(1)} %sub.53), kind=kLoop, calls=%fused_computation.12 | loop fusion | flops 6291456 | bytes 10488832 | tf_op jit(solution)/shard_map/convert_element_type | solution.py:108
  134.9 3.8 all-to-all-start
  139.4 37.0 %all-to-all-done = bf16[2,128,8,512]{1,3,0,2:T(8,128)(2,1)S(1)} async-done(((bf16[2,128,8,512]{1,3,0,2:T(8,128)(2,1)}), bf16[2,128,8,512]{1,3,0,2:T(8,128)(2,1)S(1)}, u32[]{:S(2)}, u32[]{:S(2)}) %all-to-all-start) | async-done | bytes 2097184 | tf_op jit(solution)/shard_map/all_to_all | solution.py:109
  176.4 3.5 copy.42
  179.9 3.2 all_to_all.16
  186.4 11.5 %all-gather.2 = bf16[2,1,128]{2,1,0:T(2,128)(2,1)S(1)} all-gather(bf16[1,1,128]{2,1,0:T(2,128)(2,1)S(1)} %bitcast.146), channel_id=1, replica_groups=mesh['band'=16,'chan'=2] {'chan'}, dimensions={0}, use_global_device_ids=true | all-gather | bytes 768 | tf_op jit(solution)/shard_map/all_gather | solution.py:112
  198.0 4.2 %all-gather.3 = bf16[2,1,128]{2,1,0:T(2,128)(2,1)S(1)} all-gather(bf16[1,1,128]{2,1,0:T(2,128)(2,1)S(1)} %bitcast.147), channel_id=1, replica_groups=mesh['band'=16,'chan'=2] {'chan'}, dimensions={0}, use_global_device_ids=true | all-gather | bytes 768 | tf_op jit(solution)/shard_map/all_gather | solution.py:113
  202.2 4.2 %all-gather.4 = bf16[2,1,128]{2,1,0:T(2,128)(2,1)S(1)} all-gather(bf16[1,1,128]{2,1,0:T(2,128)(2,1)S(1)} %bitcast.148), channel_id=1, replica_groups=mesh['band'=16,'chan'=2] {'chan'}, dimensions={0}, use_global_device_ids=true | all-gather | bytes 768 | tf_op jit(solution)/shard_map/all_gather | solution.py:115
  206.4 4.9 %all_gather.30 = bf16[256,256]{1,0:T(8,128)(2,1)S(1)} all-gather(bf16[128,256]{1,0:T(8,128)(2,1)S(1)} %copy-done.4), channel_id=1, replica_groups=mesh['band'=16,'chan'=2] {'chan'}, dimensions={0}, use_global_device_ids=true | all-gather | bytes 196608 | tf_op jit(solution)/shard_map/all_gather | solution.py:114
  214.5 2.7 fusion.7
  217.2 9.8 %collective-permute-done.3 = bf16[2,256,1,512]{1,3,2,0:T(8,128)(2,1)S(1)} collective-permute-done((bf16[2,256,1,512]{1,3,2,0:T(8,128)(2,1)}, bf16[2,256,1,512]{1,3,2,0:T(8,128)(2,1)S(1)}, u32[]{:S(2)}, u32[]{:S(2)}) %collective-permute-start.3) | collective-permute-done | bytes 524320 | tf_op jit(solution)/shard_map/ppermute | solution.py:27
  227.9 2.7 fusion.11
  230.6 2.7 fusion.19
  233.3 2.7 fusion.21
  236.0 2.7 fusion.23
  238.7 2.7 fusion.25
  241.5 2.8 fusion.27
  244.9 11.3 %bitcast_reduce_fusion = (f32[2,256]{1,0:T(2,128)S(1)}, f32[2,4,512,256]{3,2,1,0:T(8,128)}) fusion(bf16[3,3,256,256]{3,2,1,0:T(8,128)(2,1)} %all-gather.10.cloned.1.call-done, bf16[2,256,6,514]{1,3,2,0:T(8,128)(2,1)S(1)} %fusion.6, f32[2,4,512,256]{3,2,1,0:T(8,128)} %fusion.11, f32[2,4,512,256]{3,2,1,0:T(8,128)} %fusion.19, f32[2,4,512,256]{3,2,1,0:T(8,128)} %fusion.21, ...), kind=kOutput, calls=%fused_computation.5 | convolution fusion | flops 546307584 | bytes 39979008 | tf_op jit(solution)/shard_map/oc,ncrw->norw/dot_general | solution.py:52
  256.4 37.0 %psum.23 = f32[2,32]{1,0:T(2,128)S(1)} all-reduce(f32[2,32]{1,0:T(2,128)S(1)} %reduce_sum.90), channel_id=1, replica_groups=mesh['band'=16,'chan'=2] {'band','chan'}, use_global_device_ids=true, to_apply=%region_8.9 | all-reduce | flops 64 | bytes 512 | tf_op jit(solution)/shard_map/psum | solution.py:123
  296.4 66.1 %all-gather.1 = f32[32,2,32]{2,1,0:T(2,128)S(1)} all-gather(f32[1,2,32]{2,1,0:T(2,128)S(1)} %bitcast.142), channel_id=2, replica_groups=mesh['band'=16,'chan'=2] {'band','chan'}, dimensions={0}, use_global_device_ids=true | all-gather | bytes 8448 | tf_op jit(solution)/shard_map/all_gather | solution.py:13
  362.7 3.7 fusion.33
  366.4 2.9 exponential_reduce_fusion
  369.8 3.8 %copy.27 = f32[2,200,4,512]{3,2,1,0:T(4,128)} copy(f32[2,200,4,512]{3,1,2,0:T(8,128)S(1)} %log_subtract_fusion) | data formatting | bytes 6553600 | tf_op jit(solution)/shard_map/sub | solution.py:134
  (74 shorter events, 26.3 us)
Async XLA Ops:
  6.5 356.2 %copy-start = (bf16[200,256]{1,0:T(8,128)(2,1)S(1)}, bf16[200,256]{1,0:T(8,128)(2,1)}, u32[]{:S(2)}) copy-start(bf16[200,256]{1,0:T(8,128)(2,1)} %param.21) | copy-start | bytes 307204
  6.5 3.2 copy-start.2
  6.5 7.3 %copy-start.6 = (bf16[128]{0:T(256)(128)(2,1)S(1)}, bf16[128]{0:T(256)(128)(2,1)}, u32[]{:S(2)}) copy-start(bf16[128]{0:T(256)(128)(2,1)} %param.14) | copy-start | bytes 772
  6.5 7.3 %copy-start.7 = (bf16[128]{0:T(256)(128)(2,1)S(1)}, bf16[128]{0:T(256)(128)(2,1)}, u32[]{:S(2)}) copy-start(bf16[128]{0:T(256)(128)(2,1)} %param.15) | copy-start | bytes 772
  6.5 51.0 %all-gather.8.cloned.1.call-start = ((), (), s32[]{:S(2)}) async-start(), calls=%async_computation.1 | async-start | bytes 4718592 | tf_op jit(solution)/shard_map/all_gather | solution.py:93
  10.1 3.8 collective-permute-start
  12.6 5.5 %collective-permute-start.1 = (bf16[2,128,1,256]{3,2,1,0:T(2,128)(2,1)S(1)}, bf16[2,128,1,256]{3,2,1,0:T(2,128)(2,1)S(1)}, u32[]{:S(2)}, u32[]{:S(2)}) collective-permute-start(bf16[2,128,1,256]{3,2,1,0:T(2,128)(2,1)S(1)} %get-tuple-element.16), channel_id=1, source_target_pairs={{2,0},{4,2},{6,4},{8,6},{10,8},{12,10},{14,12},{16,14},{18,16},{20... | collective-permute-start | bytes 393224 | tf_op jit(solution)/shard_map/ppermute | solution.py:27
  28.8 28.8 %copy-start.5 = (bf16[128,192]{0,1:T(8,128)(2,1)S(1)}, bf16[128,192]{0,1:T(8,128)(2,1)}, u32[]{:S(2)}) copy-start(bf16[128,192]{0,1:T(8,128)(2,1)} %param.13) | copy-start | bytes 147460
  134.9 41.5 %all-to-all-start = ((bf16[2,128,8,512]{1,3,0,2:T(8,128)(2,1)}), bf16[2,128,8,512]{1,3,0,2:T(8,128)(2,1)S(1)}, u32[]{:S(2)}, u32[]{:S(2)}) async-start(bf16[2,128,8,512]{1,3,0,2:T(8,128)(2,1)} %copy.24), calls=%async_computation | async-start | bytes 4194304 | tf_op jit(solution)/shard_map/all_to_all | solution.py:109
  138.6 74.0 %all-gather.10.cloned.1.call-start = ((), (), s32[]{:S(2)}) async-start(), calls=%async_computation.2 | async-start | bytes 1769472 | tf_op jit(solution)/shard_map/all_gather | solution.py:111
  179.9 6.5 %copy-start.8 = (bf16[128]{0:T(256)(128)(2,1)S(1)}, bf16[128]{0:T(256)(128)(2,1)}, u32[]{:S(2)}) copy-start(bf16[128]{0:T(256)(128)(2,1)} %param.17) | copy-start | bytes 772
  179.9 18.1 %copy-start.9 = (bf16[128]{0:T(256)(128)(2,1)S(1)}, bf16[128]{0:T(256)(128)(2,1)}, u32[]{:S(2)}) copy-start(bf16[128]{0:T(256)(128)(2,1)} %param.18) | copy-start | bytes 772
  179.9 22.3 %copy-start.10 = (bf16[128]{0:T(256)(128)(2,1)S(1)}, bf16[128]{0:T(256)(128)(2,1)}, u32[]{:S(2)}) copy-start(bf16[128]{0:T(256)(128)(2,1)} %param.20) | copy-start | bytes 772
  179.9 26.6 %copy-start.4 = (bf16[128,256]{1,0:T(8,128)(2,1)S(1)}, bf16[128,256]{1,0:T(8,128)(2,1)}, u32[]{:S(2)}) copy-start(bf16[128,256]{1,0:T(8,128)(2,1)} %param.19) | copy-start | bytes 196612
  184.2 30.2 %collective-permute-start.2 = (bf16[2,256,1,512]{1,3,2,0:T(8,128)(2,1)}, bf16[2,256,1,512]{1,3,2,0:T(8,128)(2,1)S(1)}, u32[]{:S(2)}, u32[]{:S(2)}) collective-permute-start(bf16[2,256,1,512]{1,3,2,0:T(8,128)(2,1)} %get-tuple-element.9), channel_id=1, source_target_pairs={{0,1},{1,2},{2,3},{3,4},{4,5},{5,6},{6,7},{7,8},{8,9},{9,10},{10,1... | collective-permute-start | bytes 1572872 | tf_op jit(solution)/shard_map/ppermute | solution.py:25
  211.4 15.6 %collective-permute-start.3 = (bf16[2,256,1,512]{1,3,2,0:T(8,128)(2,1)}, bf16[2,256,1,512]{1,3,2,0:T(8,128)(2,1)S(1)}, u32[]{:S(2)}, u32[]{:S(2)}) collective-permute-start(bf16[2,256,1,512]{1,3,2,0:T(8,128)(2,1)} %get-tuple-element.10), channel_id=1, source_target_pairs={{1,0},{2,1},{3,2},{4,3},{5,4},{6,5},{7,6},{8,7},{9,8},{10,9},{11,1... | collective-permute-start | bytes 1572872 | tf_op jit(solution)/shard_map/ppermute | solution.py:27
  212.7 1.8 copy-start.3
  241.5 3.4 copy-start.1
Sparse Core Ops, SparseCore 0:
  9.9 47.6 all-gather.7
  141.0 33.2 all-gather.9
